TPU v7x, 32 devices: a whole 2x2x4 slice. The times are simulated.
32 devices in a mesh: batch: 4 (over y, x), seq: 4 (over z), head: 2 (over core).
Axes of the slice: x: 2, y: 2, z: 4, core: 2. Of those that a mesh axis runs over, the one named last changes fastest.
Arguments:
- queries: bfloat16 [1, 6144, 2048], P(None, ('batch', 'seq'), 'head'), parts along dimension 1, may hold values from -240 to 240
- keys: bfloat16 [1, 6144, 1024], P(None, ('batch', 'seq'), 'head'), parts along dimension 1, may hold values from -6 to 6
- values: bfloat16 [1, 6144, 1024], P(None, ('batch', 'seq'), 'head'), parts along dimension 1, may hold values from -6 to 6
- exit_layer: int32 [48], P(('batch', 'seq')), parts along dimension 0, may hold values from 0 to 1
- tile_order: int32 [48], P('batch'), parts along dimension 0, may hold values from 0 to 11, each once
Outputs:
- attended: bfloat16 [1, 6144, 2048], P(None, ('batch', 'seq'), 'head'), parts along dimension 1
- live_tiles: int32 [4], P('batch'), parts along dimension 0
There are 4 independent parts, one for each index of `batch`. A program takes and returns all parts, laid end to end along the dimension named above; each array names one. Nothing has to cross between parts.
Inputs may be any that keep to these rules, and one draw needn't show every extreme that they name: Tile t covers tokens t * 128 to t * 128 + 127 of the token dimension; tile_order is a permutation of 0 to 11.
All inputs are finite; a program needn't handle non-finite values.
Results may differ from a plain program's by a relative error of at most 0.0049.
Values may be sent and summed in bfloat16 or wider, within the bound.
A program may use at most 128 MiB of HBM per device.

v0:
```python
import functools
import math

import jax
import jax.numpy as jnp
from jax import lax
from jax.experimental import pallas as pl
from jax.experimental.pallas import tpu as pltpu
from jax.sharding import PartitionSpec as P

HD = 256
TILE = 128
SOFTCAP = 50.0
QUERY_SCALE = 0.0625
IN_SCALE = QUERY_SCALE / SOFTCAP
OUT_SCALE = SOFTCAP * math.log2(math.e)
MESH = pl.DeviceIdType.MESH


def kernel(
    n, order_ref, exit_ref, exits_vec, q_hbm, k_hbm, v_hbm, out_ref, live_ref,
    qb, kv, acc, den, done, exits, kv_sem, q_sem, send_sem, recv_sem,
    q_send, q_recv, o_send, o_recv, exit_send, exit_recv,
):
    me = lax.axis_index("seq")
    core = lax.axis_index("head")
    tiles = kv.shape[2]
    heads, rows = qb.shape[1:3]
    q_half = heads * HD
    kv_half = kv.shape[5]
    at_end = (me == 0) | (me == n - 1)
    serves = (me == 1) | (me == n - 2)
    end = jnp.where(me < n // 2, 0, n - 1)
    inward = jnp.where(me < n // 2, 1, -1)

    def peer(step):
        return {"seq": jnp.clip(me + step, 0, n - 1)}

    def own_copy(hh, t, which):
        src = (k_hbm, v_hbm)[which]
        return pltpu.make_async_copy(
            src.at[pl.ds(t * TILE, TILE), pl.ds(pl.multiple_of(hh * kv_half, kv_half), kv_half)],
            kv.at[me, hh, t, which],
            kv_sem.at[hh, t, which],
        )

    def own_queries(hh, h):
        return pltpu.make_async_copy(
            q_hbm.at[:, pl.ds(hh * q_half + h * HD, HD)], qb.at[hh, h], q_sem.at[hh, h]
        )

    first = core
    for h in range(heads):
        own_queries(0, h).start()
    for hh in (first, 1 - first):
        for t in range(tiles):
            for which in range(2):
                own_copy(hh, t, which).start()
    for h in range(heads):
        own_queries(1, h).start()

    barrier = pltpu.get_barrier_semaphore()
    for d in range(1, n):
        pl.semaphore_signal(
            barrier, inc=1, device_id={"seq": lax.rem(me + d, n)}, device_id_type=MESH
        )
    pl.semaphore_wait(barrier, n - 1)

    def hop(owner, hh, t, step):
        return pltpu.make_async_remote_copy(
            src_ref=kv.at[owner, hh, t],
            dst_ref=kv.at[owner, hh, t],
            send_sem=send_sem.at[(step + 1) // 2, owner, hh, t],
            recv_sem=recv_sem.at[owner, hh, t],
            device_id=peer(step),
            device_id_type=MESH,
        )

    def goes(hh, step):
        room = jnp.where(step > 0, n - 1 - me, me)
        return (room > 1) | ((room == 1) & (hh == 1))

    def send(owner, hh, t, step):
        @pl.when(goes(hh, step))
        def _():
            hop(owner, hh, t, step).start()

    def query_copy(t):
        part = pl.ds(t * TILE, TILE)
        return pltpu.make_async_remote_copy(
            src_ref=qb.at[0, :, part], dst_ref=qb.at[2, :, part],
            send_sem=q_send.at[t], recv_sem=q_recv.at[t],
            device_id=peer(inward), device_id_type=MESH,
        )

    def done_copy(t):
        part = pl.ds(t * TILE, TILE)
        return pltpu.make_async_remote_copy(
            src_ref=done.at[0, part], dst_ref=done.at[1, part],
            send_sem=o_send.at[t], recv_sem=o_recv.at[t],
            device_id=peer(-inward), device_id_type=MESH,
        )

    for h in range(heads):
        own_queries(0, h).wait()

    for t in range(tiles):
        for which in range(2):
            own_copy(first, t, which).wait()
        send(me, first, t, inward)
        send(me, first, t, -inward)

    @pl.when(at_end)
    def _():
        for t in range(tiles):
            query_copy(t).start()

    def exit_copy(d):
        return pltpu.make_async_remote_copy(
            src_ref=exits_vec, dst_ref=exits.at[d - 1],
            send_sem=exit_send.at[d - 1], recv_sem=exit_recv.at[d - 1],
            device_id={"seq": lax.rem(me + d, n)}, device_id_type=MESH,
        )

    for t in range(tiles):
        for which in range(2):
            own_copy(1 - first, t, which).wait()
        send(me, 1 - first, t, -inward)

        @pl.when(at_end)
        def _():
            send(me, 1 - first, t, inward)

    for d in range(1, n):
        exit_copy(d).start()

    acc[...] = jnp.zeros_like(acc)
    den[...] = jnp.zeros_like(den)
    for h in range(heads):
        own_queries(1, h).wait()
    ahead = lax.broadcasted_iota(jnp.int32, (TILE, TILE), 1) - lax.broadcasted_iota(
        jnp.int32, (TILE, TILE), 0
    )

    def fold_into(slot, row_owner, owner, hh, t):
        key_place = order_ref[owner * tiles + t]
        over = jnp.stack(
            [
                ahead - (order_ref[row_owner * tiles + i] - key_place) * TILE
                for i in range(tiles)
            ]
        )
        stacked = (heads * rows, HD)
        scores = lax.dot_general(
            qb[slot].reshape(stacked), kv[owner, hh, t, 0],
            (((1,), (1,)), ((), ())), preferred_element_type=jnp.float32,
        ).reshape(heads, tiles, TILE, TILE)
        weights = jnp.where(
            over[None] <= 0, jnp.exp2(OUT_SCALE * jnp.tanh(scores * IN_SCALE)), 0.0
        ).reshape(heads * rows, TILE)
        den[slot] += weights
        acc[slot] += jnp.dot(
            weights.astype(jnp.bfloat16), kv[owner, hh, t, 1],
            preferred_element_type=jnp.float32,
        )

    def fold(owner, hh, t, phase):
        low = jnp.where(at_end & (hh == 0), 1, 0)
        high = jnp.where(serves & (hh == 0) & (phase == 1), 2, 1)

        @pl.loop(low, high)
        def _(k):
            fold_into(
                jnp.where(k == 0, hh, 2), jnp.where(k == 0, me, end), owner, hh, t
            )

    def finish(slot, i, h):
        here = pl.ds(h * rows + i * TILE, TILE)
        total = jnp.sum(den[slot, here, :], axis=1, keepdims=True)
        return (acc[slot, here, :] / total).astype(jnp.bfloat16)

    def keep(slot, i, h):
        out_ref[pl.ds(i * TILE, TILE), pl.ds(slot * q_half + h * HD, HD)] = live_only(
            i, finish(slot, i, h)
        )

    def live_only(i, rows_out):
        return jnp.where(exit_ref[i] > 0, rows_out, jnp.zeros_like(rows_out))

    def late_fold(part, parts):
        share = n * tiles // parts

        @pl.loop(part * share, (part + 1) * share)
        def _(k):
            fold_into(2, end, k // tiles, 0, k % tiles)

    def finish_served():
        for t in range(tiles):
            for h in range(heads):
                done[0, pl.ds(t * TILE, TILE), pl.ds(h * HD, HD)] = finish(2, t, h)
            if t > 0:
                done_copy(t - 1).start()
        for h in range(heads):
            keep(0, 0, h)
        done_copy(tiles - 1).start()

    def arrive(owner, hh, t, side, phase):
        @pl.when((owner >= 0) & (owner < n) & ~(at_end & (hh == 0)))
        def _():
            hop(owner, hh, t, side).wait_recv()
            send(owner, hh, t, -side)

    def take(owner, hh, t, phase):
        @pl.when((owner >= 0) & (owner < n) & ~(at_end & (hh == 0)))
        def _():
            fold(owner, hh, t, phase)

    near = []
    for s in (1, 2):
        for t in range(tiles):
            near.append((tiles * (s - 1) + t + 1.0, 1, s, t))
            if s == 1 or n > 4:
                near.append((tiles * 2 * (s - 1) + 2 * t + 1.1, -1, s, t))
    near.sort()

    @pl.loop(0, 2)
    def _(phase):
        hh = jnp.where(phase == 0, first, 1 - first)

        @pl.when(serves & (phase == 1))
        def _():
            for t in range(tiles):
                query_copy(t).wait_recv()

        @pl.loop(0, tiles)
        def _(t):
            fold(me, hh, t, phase)

            @pl.when(serves & (phase == 1) & (core == 0))
            def _():
                late_fold(t, 2 * tiles)

        for _, sign, s, t in near:
            side = inward * sign
            owner = me + side * s
            arrive(owner, hh, t, side, phase)
            if sign == -1 and s == 1:
                if t == tiles - 1:
                    @pl.when((phase == 0) & ~at_end)
                    def _():
                        for own_t in range(tiles):
                            send(me, 1 - first, own_t, inward)
            take(owner, hh, t, phase)
            if sign == 1 and s == 1:
                @pl.when(serves & (phase == 1) & (core == 0))
                def _():
                    late_fold(tiles + t, 2 * tiles)

                    if t == tiles - 1:
                        finish_served()

        @pl.loop(3, n)
        def _(s):
            @pl.loop(0, tiles)
            def _(t):
                for sign in (1, -1) if n > 4 else (1,):
                    side = inward * sign
                    arrive(me + side * s, hh, t, side, phase)
                    take(me + side * s, hh, t, phase)

        @pl.when(serves & (hh == 0) & (phase == 1))
        def _():
            finish_served()

    for i in range(rows // TILE):
        for h in range(heads):
            keep(1, i, h)

    @pl.when(~at_end)
    def _():
        for i in range(rows // TILE):
            for h in range(heads):
                keep(0, i, h)

    count = jnp.sum((exits_vec[...] > 0).astype(jnp.int32))
    for d in range(1, n):
        exit_copy(d).wait()
        count += jnp.sum((exits[d - 1] > 0).astype(jnp.int32))
    live_ref[0] = count

    @pl.when(at_end)
    def _():
        for t in range(tiles):
            here = pl.ds(t * TILE, TILE)
            done_copy(t).wait_recv()
            out_ref[here, pl.ds(0, q_half)] = live_only(t, done[1, here, :])
            query_copy(t).wait_send()

    @pl.when(serves)
    def _():
        for t in range(tiles):
            done_copy(t).wait_send()

    for step in (1, -1):
        @pl.loop(0, n)
        def _(s):
            owner = me - step * s

            @pl.loop(0, 2)
            def _(hh):
                @pl.when((owner >= 0) & (owner < n) & goes(hh, step))
                def _():
                    @pl.loop(0, tiles)
                    def _(t):
                        hop(owner, hh, t, step).wait_send()


def body(n, queries, keys, values, exit_layer, tile_order):
    rows, q_width = queries.shape[1:]
    kv_half = keys.shape[2] // 2
    q_half = q_width // 2
    tiles = rows // TILE
    exits_vec = jnp.pad(exit_layer, (0, TILE - tiles)).reshape(1, TILE)
    smem = pl.BlockSpec(memory_space=pltpu.SMEM)
    hbm = pl.BlockSpec(memory_space=pl.ANY)
    vmem = pl.BlockSpec(memory_space=pltpu.VMEM)
    dma = pltpu.SemaphoreType.DMA
    attended, live = pl.pallas_call(
        functools.partial(kernel, n),
        out_shape=(
            jax.ShapeDtypeStruct((rows, q_width), jnp.bfloat16),
            jax.ShapeDtypeStruct((1,), jnp.int32),
        ),
        in_specs=[smem, smem, vmem, hbm, hbm, hbm],
        out_specs=(vmem, smem),
        scratch_shapes=[
            pltpu.VMEM((3, q_half // HD, rows, HD), jnp.bfloat16),
            pltpu.VMEM((n, 2, tiles, 2, TILE, kv_half), jnp.bfloat16),
            pltpu.VMEM((3, rows * q_half // HD, HD), jnp.float32),
            pltpu.VMEM((3, rows * q_half // HD, TILE), jnp.float32),
            pltpu.VMEM((2, rows, q_half), jnp.bfloat16),
            pltpu.VMEM((n - 1, 1, TILE), jnp.int32),
            dma((2, tiles, 2)),
            dma((2, q_half // HD)),
            dma((2, n, 2, tiles)),
            dma((n, 2, tiles)),
            dma((tiles,)),
            dma((tiles,)),
            dma((tiles,)),
            dma((tiles,)),
            dma((n - 1,)),
            dma((n - 1,)),
        ],
        compiler_params=pltpu.CompilerParams(
            collective_id=0, has_side_effects=True, vmem_limit_bytes=64_000_000
        ),
        name="attend_line",
    )(tile_order, exit_layer, exits_vec, queries[0], keys[0], values[0])
    return attended[None], live


def solution(mesh):
    return jax.shard_map(
        functools.partial(body, mesh.shape["seq"]),
        mesh=mesh,
        in_specs=(
            P(None, ("batch", "seq"), "head"),
            P(None, ("batch", "seq"), "head"),
            P(None, ("batch", "seq"), "head"),
            P(("batch", "seq")),
            P("batch"),
        ),
        out_specs=(P(None, ("batch", "seq"), "head"), P("batch")),
        check_vma=False,
    )
```

profile of v0, /device:TPU:0, one launch (start us, length us, event | category | flops | bytes accessed | tf_op | source)
XLA Modules:
  0.0 61.1 jit_solution(6247954407073155479)
XLA Ops:
  0.6 0.0 copy-start
  0.6 0.6 %copy-done = s32[3]{0:T(128)S(1)} copy-done((s32[3]{0:T(128)S(1)}, s32[3]{0:T(128)}, u32[]{:S(2)}) %copy-start) | copy-done | bytes 36
  1.3 0.5 pad_bitcast_fusion.exits_vec
  1.8 55.4 %attend_line.1 = (bf16[384,1024]{1,0:T(8,128)(2,1)}, s32[1]{0:T(128)}) custom-call(s32[12]{0:T(128)} %order_ref.1, s32[3]{0:T(128)} %exit_ref.1, s32[1,128]{1,0:T(1,128)} %pad_bitcast_fusion.exits_vec, bf16[384,1024]{1,0:T(8,128)(2,1)} %bitcast.6, bf16[384,512]{1,0:T(8,128)(2,1)} %bitcast.8, bf16[384,512]{1,0:T(8,128)(2,1)} %bitcast.9), custom_call_target="tpu_custom_call" | custom-call | tf_op jit(solution)/shard_map/attend_line/pallas_call | solution.py:328
  57.2 2.1 %copy.9 = bf16[1,384,1024]{2,1,0:T(8,128)(2,1)} copy(bf16[1,384,1024]{2,1,0:T(8,128)(2,1)} %bitcast.7) | data formatting | bytes 1572864
Async XLA Ops:
  0.6 0.7 %copy-start = (s32[3]{0:T(128)S(1)}, s32[3]{0:T(128)}, u32[]{:S(2)}) copy-start(s32[3]{0:T(128)} %exit_ref.1) | copy-start | bytes 40
where the time goes:
time: 61.3 us; the launch traced here: 61.1 us
  Pallas kernels  55.4 us (90%)
  local copies, waits for them, and re-layouts  3.23 us (5%)
  between operations  2.41 us (4%)
    pallas_call x1, Pallas kernels, body(): pl.pallas_call(functools.partial(kernel, n), out_shape=(jax.ShapeDtypeStr...  55.4 us
    unnamed x3, local copies, waits for them, and re-layouts  2.71 us

commit v1 on v0

v1 whole, which is shorter than its diff:
```python
import functools
import math

import jax
import jax.numpy as jnp
from jax import lax
from jax.experimental import pallas as pl
from jax.experimental.pallas import tpu as pltpu
from jax.sharding import PartitionSpec as P

HD = 256
TILE = 128
SOFTCAP = 50.0
QUERY_SCALE = 0.0625
IN_SCALE = QUERY_SCALE / SOFTCAP
OUT_SCALE = SOFTCAP * math.log2(math.e)
MESH = pl.DeviceIdType.MESH
SERVED, SPREAD = 0, 1


def kernel(
    n, order_ref, exit_ref, q_hbm, k_hbm, v_hbm, out_ref, live_ref,
    qb, kv, acc, den, done, exits, kv_sem, q_sem, send_sem, recv_sem,
    pair_send, pair_recv, exit_send, exit_recv,
):
    me = lax.axis_index("seq")
    core = lax.axis_index("head")
    tiles = kv.shape[2]
    heads, rows = qb.shape[1:3]
    q_half = heads * HD
    far = n - 1
    at_end = (me == 0) | (me == far)
    serves = (me == 1) | (me == far - 1)
    end = jnp.where(me < n // 2, 0, far)
    inward = jnp.where(me < n // 2, 1, -1)
    first = core

    def inside(owner):
        return (owner >= 0) & (owner < n)

    def peer(step):
        return {"seq": jnp.clip(me + step, 0, far)}

    def own_copy(hh, which):
        src = (k_hbm, v_hbm)[which]
        return pltpu.make_async_copy(
            src.at[:, :, pl.ds(pl.multiple_of(hh * HD, HD), HD)],
            kv.at[me, hh, :, which],
            kv_sem.at[hh, which],
        )

    def own_queries(hh, h):
        return pltpu.make_async_copy(
            q_hbm.at[:, pl.ds(hh * q_half + h * HD, HD)], qb.at[hh, h], q_sem.at[hh, h]
        )

    barrier = pltpu.get_barrier_semaphore()
    for step in (1, -1):
        @pl.when(inside(me + step))
        def _():
            pl.semaphore_signal(barrier, inc=1, device_id=peer(step), device_id_type=MESH)

    for which in range(2):
        own_copy(first, which).start()
    for h in range(heads):
        own_queries(0, h).start()
    for which in range(2):
        own_copy(1 - first, which).start()
    for h in range(heads):
        own_queries(1, h).start()

    lane = lax.broadcasted_iota(jnp.int32, (1, TILE), 1)
    mine = jnp.zeros((1, TILE), jnp.int32)
    for i in range(tiles):
        mine = jnp.where(lane == i, exit_ref[i], mine)
    exits[me] = mine

    pl.semaphore_wait(barrier, jnp.where(at_end, 1, 2))

    def hop(owner, hh, t, step):
        return pltpu.make_async_remote_copy(
            src_ref=kv.at[owner, hh, t],
            dst_ref=kv.at[owner, hh, t],
            send_sem=send_sem.at[jnp.where((owner == me) & (step < 0), n, owner), hh, t],
            recv_sem=recv_sem.at[owner, hh, t],
            device_id=peer(step),
            device_id_type=MESH,
        )

    def exit_hop(owner, step):
        return pltpu.make_async_remote_copy(
            src_ref=exits.at[owner],
            dst_ref=exits.at[owner],
            send_sem=exit_send.at[jnp.where((owner == me) & (step < 0), n, owner)],
            recv_sem=exit_recv.at[owner],
            device_id=peer(step),
            device_id_type=MESH,
        )

    def goes(hh, step):
        room = jnp.where(step > 0, far - me, me)
        return (room > 1) | ((room == 1) & (hh == SPREAD))

    def send(owner, hh, t, step):
        @pl.when(goes(hh, step))
        def _():
            hop(owner, hh, t, step).start()

    def send_own(hh, step):
        @pl.loop(0, tiles)
        def _(t):
            send(me, hh, t, step)

    def query_copy():
        return pltpu.make_async_remote_copy(
            src_ref=qb.at[0], dst_ref=qb.at[2],
            send_sem=pair_send.at[tiles], recv_sem=pair_recv.at[tiles],
            device_id=peer(inward), device_id_type=MESH,
        )

    def done_copy(t):
        part = pl.ds(t * TILE, TILE)
        return pltpu.make_async_remote_copy(
            src_ref=done.at[0, part], dst_ref=done.at[1, part],
            send_sem=pair_send.at[t], recv_sem=pair_recv.at[t],
            device_id=peer(-inward), device_id_type=MESH,
        )

    def wait_own(hh):
        for which in range(2):
            own_copy(hh, which).wait()

    @pl.when(at_end & (core == 0))
    def _():
        for h in range(heads):
            own_queries(0, h).wait()
        query_copy().start()

    wait_own(first)

    @pl.when(~at_end)
    def _():
        send_own(first, inward)
        send_own(first, -inward)

    @pl.when(at_end & (core == 0))
    def _():
        send_own(SERVED, inward)

    wait_own(1 - first)

    @pl.when(~at_end)
    def _():
        send_own(1 - first, -inward)

        @pl.when(core == 1)
        def _():
            send_own(SERVED, inward)

    @pl.when(at_end & (core == 0))
    def _():
        send_own(SPREAD, inward)

    for step in (1, -1):
        @pl.when(inside(me + step))
        def _():
            exit_hop(me, step).start()

    acc[...] = jnp.zeros_like(acc)
    den[...] = jnp.zeros_like(den)

    @pl.when(~(at_end & (core == 0)))
    def _():
        for h in range(heads):
            own_queries(0, h).wait()
    for h in range(heads):
        own_queries(1, h).wait()
    ahead = lax.broadcasted_iota(jnp.int32, (TILE, TILE), 1) - lax.broadcasted_iota(
        jnp.int32, (TILE, TILE), 0
    )

    def fold_into(slot, row_owner, owner, hh, t):
        key_place = order_ref[owner * tiles + t]
        over = jnp.stack(
            [
                ahead - (order_ref[row_owner * tiles + i] - key_place) * TILE
                for i in range(tiles)
            ]
        )
        stacked = (heads * rows, HD)
        scores = lax.dot_general(
            qb[slot].reshape(stacked), kv[owner, hh, t, 0],
            (((1,), (1,)), ((), ())), preferred_element_type=jnp.float32,
        ).reshape(heads, tiles, TILE, TILE)
        weights = jnp.where(
            over[None] <= 0, jnp.exp2(OUT_SCALE * jnp.tanh(scores * IN_SCALE)), 0.0
        ).reshape(heads * rows, TILE)
        den[slot] += weights
        acc[slot] += jnp.dot(
            weights.astype(jnp.bfloat16), kv[owner, hh, t, 1],
            preferred_element_type=jnp.float32,
        )

    def finish(slot, i, h):
        here = pl.ds(h * rows + i * TILE, TILE)
        total = jnp.sum(den[slot, here, :], axis=1, keepdims=True)
        return (acc[slot, here, :] / total).astype(jnp.bfloat16)

    def live_only(i, rows_out):
        return jnp.where(exit_ref[i] > 0, rows_out, jnp.zeros_like(rows_out))

    def keep(slot, i, h):
        out_ref[pl.ds(i * TILE, TILE), pl.ds(slot * q_half + h * HD, HD)] = live_only(
            i, finish(slot, i, h)
        )

    @pl.loop(jnp.where(at_end, tiles * (1 - core), 0), jnp.where(at_end, tiles * (2 - core), 2 * tiles))
    def _(k):
        hh = jnp.where(k < tiles, first, 1 - first)
        fold_into(hh, me, me, hh, lax.rem(k, tiles))

    def arrive(owner, hh, t, side):
        hop(owner, hh, t, side).wait_recv()
        send(owner, hh, t, -side)

        @pl.when((hh == SPREAD) & (t == 0))
        def _():
            exit_hop(owner, side).wait_recv()

            @pl.when(inside(me - side))
            def _():
                exit_hop(owner, -side).start()

    early = core == 0

    @pl.loop(0, 2 * far)
    def _(u):
        hh_in = jnp.where(early, u >= far, (u == 0) | (u > far)).astype(jnp.int32)
        s_in = jnp.where(
            u >= far + 1 - early, u - far + 1, jnp.where(early, u + 1, jnp.maximum(u, 1))
        )
        hh_out = (u >= far).astype(jnp.int32)
        s_out = jnp.where(u >= far, u - far + 1, u + early)
        from_in = me + inward * s_in
        from_out = me - inward * s_out
        has_in = inside(from_in) & ~(at_end & (hh_in == SERVED))
        has_out = inside(from_out) & (s_out > 0) & ~at_end
        serving = serves & (hh_in == SERVED)

        @pl.when(serving & (s_in == 2))
        def _():
            query_copy().wait_recv()

        @pl.loop(0, tiles)
        def _(t):
            @pl.when(at_end & (u == 2 * far - 1) & (t == tiles - 1))
            def _():
                for i in range(tiles):
                    here = pl.ds(i * TILE, TILE)
                    done_copy(i).wait_recv()
                    out_ref[here, pl.ds(0, q_half)] = live_only(i, done[1, here, :])

            @pl.when(has_in)
            def _():
                arrive(from_in, hh_in, t, inward)

            @pl.when(has_out)
            def _():
                arrive(from_out, hh_out, t, -inward)

            @pl.loop(0, 6)
            def _(k):
                near = jnp.where(k == 3, me, jnp.where(k == 4, me + inward, me - inward))
                owner = jnp.where(k > 2, near, jnp.where(k == 1, from_out, from_in))
                runs = jnp.where(
                    k > 2,
                    serving & (s_in == 2),
                    jnp.where(k == 2, serving & has_in & (s_in > 1), jnp.where(k == 1, has_out, has_in)),
                )
                hh = jnp.where(k == 1, hh_out, hh_in)

                @pl.when(runs)
                def _():
                    fold_into(
                        jnp.where(k > 1, 2, hh), jnp.where(k > 1, end, me), owner, hh, t
                    )

        @pl.when((u == 0) & early & ~at_end)
        def _():
            send_own(SPREAD, inward)

        @pl.when((u == 0) & ~early & at_end)
        def _():
            query_copy().start()
            send_own(SERVED, inward)
            send_own(SPREAD, inward)

        @pl.when(serving & (s_in == far - 1))
        def _():
            for t in range(tiles):
                for h in range(heads):
                    done[0, pl.ds(t * TILE, TILE), pl.ds(h * HD, HD)] = finish(2, t, h)
                if t > 0:
                    done_copy(t - 1).start()
            for h in range(heads):
                keep(0, 0, h)
            done_copy(tiles - 1).start()

    for i in range(tiles):
        for h in range(heads):
            keep(1, i, h)

    @pl.when(~at_end)
    def _():
        for i in range(tiles):
            for h in range(heads):
                keep(0, i, h)

    live_ref[0] = jnp.sum((exits[...] > 0).astype(jnp.int32))

    @pl.when(at_end)
    def _():
        query_copy().wait_send()

    @pl.when(serves)
    def _():
        for t in range(tiles):
            done_copy(t).wait_send()

    for step in (1, -1):
        @pl.loop(0, n)
        def _(s):
            owner = me - step * s

            @pl.when(inside(owner) & inside(me + step))
            def _():
                exit_hop(owner, step).wait_send()

            @pl.loop(0, 2)
            def _(hh):
                @pl.when(inside(owner) & goes(hh, step))
                def _():
                    @pl.loop(0, tiles)
                    def _(t):
                        hop(owner, hh, t, step).wait_send()


def body(n, queries, keys, values, exit_layer, tile_order):
    rows, q_width = queries.shape[1:]
    kv_width = keys.shape[2]
    q_half = q_width // 2
    heads = q_half // HD
    tiles = rows // TILE
    smem = pl.BlockSpec(memory_space=pltpu.SMEM)
    hbm = pl.BlockSpec(memory_space=pl.ANY)
    vmem = pl.BlockSpec(memory_space=pltpu.VMEM)
    dma = pltpu.SemaphoreType.DMA
    attended, live = pl.pallas_call(
        functools.partial(kernel, n),
        out_shape=(
            jax.ShapeDtypeStruct((rows, q_width), jnp.bfloat16),
            jax.ShapeDtypeStruct((1,), jnp.int32),
        ),
        in_specs=[smem, smem, hbm, hbm, hbm],
        out_specs=(vmem, smem),
        scratch_shapes=[
            pltpu.VMEM((3, heads, rows, HD), jnp.bfloat16),
            pltpu.VMEM((n, 2, tiles, 2, TILE, HD), jnp.bfloat16),
            pltpu.VMEM((3, heads * rows, HD), jnp.float32),
            pltpu.VMEM((3, heads * rows, TILE), jnp.float32),
            pltpu.VMEM((2, rows, q_half), jnp.bfloat16),
            pltpu.VMEM((n, 1, TILE), jnp.int32),
            dma((2, 2)),
            dma((2, heads)),
            dma((n + 1, 2, tiles)),
            dma((n, 2, tiles)),
            dma((tiles + 1,)),
            dma((tiles + 1,)),
            dma((n + 1,)),
            dma((n,)),
        ],
        compiler_params=pltpu.CompilerParams(
            collective_id=0, has_side_effects=True, vmem_limit_bytes=64_000_000
        ),
        name="attend_line",
    )(
        tile_order, exit_layer, queries[0],
        keys.reshape(tiles, TILE, kv_width), values.reshape(tiles, TILE, kv_width),
    )
    return attended[None], live


def solution(mesh):
    return jax.shard_map(
        functools.partial(body, mesh.shape["seq"]),
        mesh=mesh,
        in_specs=(
            P(None, ("batch", "seq"), "head"),
            P(None, ("batch", "seq"), "head"),
            P(None, ("batch", "seq"), "head"),
            P(("batch", "seq")),
            P("batch"),
        ),
        out_specs=(P(None, ("batch", "seq"), "head"), P("batch")),
        check_vma=False,
    )
```

time: 61.3 us -> 57.2 us (0.933)
  the two profiles are of different devices: /device:TPU:0 before, /device:TPU:1 now
where the time goes in v1:
time: 57.2 us; the launch traced here: 57 us
  Pallas kernels  52.7 us (92%)
  between operations  2.32 us (4%)
  local copies, waits for them, and re-layouts  2.06 us (4%)
    pallas_call x1, Pallas kernels, body(): pl.pallas_call(functools.partial(kernel, n), out_shape=(jax.ShapeDtypeStr...  52.7 us
    unnamed x1, local copies, waits for them, and re-layouts  2.06 us

profile of v1, /device:TPU:1, one launch (start us, length us, event | category | flops | bytes accessed | tf_op | source)
XLA Modules:
  0.0 57.0 jit_solution(14527050797637878411)
XLA Ops:
  0.6 52.7 %attend_line.1 = (bf16[384,1024]{1,0:T(8,128)(2,1)}, s32[1]{0:T(128)}) custom-call(s32[12]{0:T(128)} %order_ref.1, s32[3]{0:T(128)} %exit_ref.1, bf16[384,1024]{1,0:T(8,128)(2,1)} %bitcast.5, bf16[3,128,512]{2,1,0:T(8,128)(2,1)} %bitcast.6, bf16[3,128,512]{2,1,0:T(8,128)(2,1)} %bitcast.7), custom_call_target="tpu_custom_call" | custom-call | tf_op jit(solution)/shard_map/attend_line/pallas_call | solution.py:358
  53.3 2.1 %copy.9 = bf16[1,384,1024]{2,1,0:T(8,128)(2,1)} copy(bf16[1,384,1024]{2,1,0:T(8,128)(2,1)} %bitcast.4) | data formatting | bytes 1572864

commit v2 on v1

--- a/solution.py
+++ b/solution.py
@@ -16,12 +16,13 @@
 OUT_SCALE = SOFTCAP * math.log2(math.e)
 MESH = pl.DeviceIdType.MESH
 SERVED, SPREAD = 0, 1
+GATE_A, GATE_B = 2, 1
 
 
 def kernel(
-    n, order_ref, exit_ref, q_hbm, k_hbm, v_hbm, out_ref, live_ref,
-    qb, kv, acc, den, done, exits, kv_sem, q_sem, send_sem, recv_sem,
-    pair_send, pair_recv, exit_send, exit_recv,
+    n, order_hbm, exit_hbm, q_hbm, k_hbm, v_hbm, out_ref, live_hbm,
+    qb, kv, acc, den, done, exits, order_ref, exit_ref, live_ref, kv_sem, q_sem,
+    small_sem, send_sem, recv_sem, pair_send, pair_recv, exit_send, exit_recv, ready,
 ):
     me = lax.axis_index("seq")
     core = lax.axis_index("head")
@@ -54,28 +55,40 @@
             q_hbm.at[:, pl.ds(hh * q_half + h * HD, HD)], qb.at[hh, h], q_sem.at[hh, h]
         )
 
+    small = [
+        pltpu.make_async_copy(exit_hbm, exit_ref, small_sem.at[0]),
+        pltpu.make_async_copy(order_hbm, order_ref, small_sem.at[1]),
+    ]
+    result = pltpu.make_async_copy(live_ref, live_hbm, small_sem.at[2])
+
     barrier = pltpu.get_barrier_semaphore()
-    for step in (1, -1):
-        @pl.when(inside(me + step))
-        def _():
-            pl.semaphore_signal(barrier, inc=1, device_id=peer(step), device_id_type=MESH)
-
+
+    @pl.when(inside(me + 1))
+    def _():
+        pl.semaphore_signal(barrier, inc=1, device_id=peer(1), device_id_type=MESH)
+
+    small[0].start()
     for which in range(2):
         own_copy(first, which).start()
     for h in range(heads):
         own_queries(0, h).start()
+    small[1].start()
     for which in range(2):
         own_copy(1 - first, which).start()
     for h in range(heads):
         own_queries(1, h).start()
 
+    small[0].wait()
     lane = lax.broadcasted_iota(jnp.int32, (1, TILE), 1)
     mine = jnp.zeros((1, TILE), jnp.int32)
     for i in range(tiles):
         mine = jnp.where(lane == i, exit_ref[i], mine)
     exits[me] = mine
 
-    pl.semaphore_wait(barrier, jnp.where(at_end, 1, 2))
+    @pl.when(inside(me - 1))
+    def _():
+        pl.semaphore_wait(barrier, 1)
+        pl.semaphore_signal(ready, inc=1, device_id=peer(-1), device_id_type=MESH)
 
     def hop(owner, hh, t, step):
         return pltpu.make_async_remote_copy(
@@ -130,51 +143,47 @@
         for which in range(2):
             own_copy(hh, which).wait()
 
-    @pl.when(at_end & (core == 0))
-    def _():
-        for h in range(heads):
-            own_queries(0, h).wait()
-        query_copy().start()
+    def open_side(step):
+        exit_hop(me, step).start()
+
+        @pl.when(~at_end)
+        def _():
+            send_own(first, step)
+
+        @pl.when(at_end & (core == 0))
+        def _():
+            query_copy().start()
+            send_own(SERVED, step)
 
     wait_own(first)
+    for h in range(heads):
+        own_queries(0, h).wait()
+
+    @pl.when(inside(me - 1))
+    def _():
+        open_side(-1)
+
+    @pl.when(inside(me + 1))
+    def _():
+        pl.semaphore_wait(ready, 1)
+        open_side(1)
+
+    wait_own(1 - first)
 
     @pl.when(~at_end)
     def _():
-        send_own(first, inward)
-        send_own(first, -inward)
-
-    @pl.when(at_end & (core == 0))
-    def _():
-        send_own(SERVED, inward)
-
-    wait_own(1 - first)
-
-    @pl.when(~at_end)
-    def _():
         send_own(1 - first, -inward)
 
         @pl.when(core == 1)
         def _():
             send_own(SERVED, inward)
-
-    @pl.when(at_end & (core == 0))
-    def _():
-        send_own(SPREAD, inward)
-
-    for step in (1, -1):
-        @pl.when(inside(me + step))
-        def _():
-            exit_hop(me, step).start()
 
     acc[...] = jnp.zeros_like(acc)
     den[...] = jnp.zeros_like(den)
 
-    @pl.when(~(at_end & (core == 0)))
-    def _():
-        for h in range(heads):
-            own_queries(0, h).wait()
     for h in range(heads):
         own_queries(1, h).wait()
+    small[1].wait()
     ahead = lax.broadcasted_iota(jnp.int32, (TILE, TILE), 1) - lax.broadcasted_iota(
         jnp.int32, (TILE, TILE), 0
     )
@@ -245,55 +254,55 @@
         from_out = me - inward * s_out
         has_in = inside(from_in) & ~(at_end & (hh_in == SERVED))
         has_out = inside(from_out) & (s_out > 0) & ~at_end
-        serving = serves & (hh_in == SERVED)
-
-        @pl.when(serving & (s_in == 2))
-        def _():
-            query_copy().wait_recv()
-
-        @pl.loop(0, tiles)
-        def _(t):
-            @pl.when(at_end & (u == 2 * far - 1) & (t == tiles - 1))
-            def _():
-                for i in range(tiles):
-                    here = pl.ds(i * TILE, TILE)
-                    done_copy(i).wait_recv()
-                    out_ref[here, pl.ds(0, q_half)] = live_only(i, done[1, here, :])
-
-            @pl.when(has_in)
-            def _():
-                arrive(from_in, hh_in, t, inward)
-
-            @pl.when(has_out)
-            def _():
-                arrive(from_out, hh_out, t, -inward)
-
-            @pl.loop(0, 6)
-            def _(k):
-                near = jnp.where(k == 3, me, jnp.where(k == 4, me + inward, me - inward))
-                owner = jnp.where(k > 2, near, jnp.where(k == 1, from_out, from_in))
-                runs = jnp.where(
-                    k > 2,
-                    serving & (s_in == 2),
-                    jnp.where(k == 2, serving & has_in & (s_in > 1), jnp.where(k == 1, has_out, has_in)),
-                )
-                hh = jnp.where(k == 1, hh_out, hh_in)
-
-                @pl.when(runs)
-                def _():
-                    fold_into(
-                        jnp.where(k > 1, 2, hh), jnp.where(k > 1, end, me), owner, hh, t
-                    )
-
-        @pl.when((u == 0) & early & ~at_end)
-        def _():
-            send_own(SPREAD, inward)
-
-        @pl.when((u == 0) & ~early & at_end)
-        def _():
-            query_copy().start()
-            send_own(SERVED, inward)
-            send_own(SPREAD, inward)
+        serving = serves & (hh_in == SERVED) & inside(from_in)
+
+        @pl.when(has_in | has_out)
+        def _():
+            @pl.loop(0, tiles)
+            def _(t):
+                @pl.when((u == 2 * far - 1) & (t == tiles - 1) & at_end)
+                def _():
+                    for i in range(tiles):
+                        here = pl.ds(i * TILE, TILE)
+                        done_copy(i).wait_recv()
+                        out_ref[here, pl.ds(0, q_half)] = live_only(i, done[1, here, :])
+
+                @pl.when(has_in)
+                def _():
+                    arrive(from_in, hh_in, t, inward)
+
+                @pl.when(has_out)
+                def _():
+                    arrive(from_out, hh_out, t, -inward)
+
+                @pl.when(early & ~at_end & (u == 0) & (t == tiles - 1))
+                def _():
+                    send_own(SPREAD, inward)
+
+                @pl.when(~early & at_end & (u == 0) & (t == GATE_B))
+                def _():
+                    query_copy().start()
+                    send_own(SERVED, inward)
+                    send_own(SPREAD, inward)
+
+                @pl.when(early & at_end & (u == far) & (t == GATE_A))
+                def _():
+                    send_own(SPREAD, inward)
+
+                @pl.when(serving & (s_in == 1) & (t == 0))
+                def _():
+                    query_copy().wait_recv()
+
+                @pl.loop(jnp.where(has_in, 0, 1), jnp.where(serving, jnp.where(s_in == 1, 5, 3), jnp.where(has_out, 2, 1)))
+                def _(k):
+                    owner = jnp.where(k == 4, me, jnp.where((k == 1) | (k == 3), from_out, from_in))
+                    hh = jnp.where(k == 1, hh_out, hh_in)
+
+                    @pl.when(has_out | (k != 1))
+                    def _():
+                        fold_into(
+                            jnp.where(k > 1, 2, hh), jnp.where(k > 1, end, me), owner, hh, t
+                        )
 
         @pl.when(serving & (s_in == far - 1))
         def _():
@@ -306,6 +315,9 @@
                 keep(0, 0, h)
             done_copy(tiles - 1).start()
 
+    live_ref[0] = jnp.sum((exits[...] > 0).astype(jnp.int32))
+    result.start()
+
     for i in range(tiles):
         for h in range(heads):
             keep(1, i, h)
@@ -315,8 +327,6 @@
         for i in range(tiles):
             for h in range(heads):
                 keep(0, i, h)
-
-    live_ref[0] = jnp.sum((exits[...] > 0).astype(jnp.int32))
 
     @pl.when(at_end)
     def _():
@@ -343,6 +353,8 @@
                     @pl.loop(0, tiles)
                     def _(t):
                         hop(owner, hh, t, step).wait_send()
+
+    result.wait()
 
 
 def body(n, queries, keys, values, exit_layer, tile_order):
@@ -351,18 +363,17 @@
     q_half = q_width // 2
     heads = q_half // HD
     tiles = rows // TILE
-    smem = pl.BlockSpec(memory_space=pltpu.SMEM)
-    hbm = pl.BlockSpec(memory_space=pl.ANY)
+    hbm = pl.BlockSpec(memory_space=pltpu.HBM)
     vmem = pl.BlockSpec(memory_space=pltpu.VMEM)
     dma = pltpu.SemaphoreType.DMA
     attended, live = pl.pallas_call(
         functools.partial(kernel, n),
         out_shape=(
-            jax.ShapeDtypeStruct((rows, q_width), jnp.bfloat16),
+            pltpu.VMEM((rows, q_width), jnp.bfloat16),
             jax.ShapeDtypeStruct((1,), jnp.int32),
         ),
-        in_specs=[smem, smem, hbm, hbm, hbm],
-        out_specs=(vmem, smem),
+        in_specs=[hbm] * 5,
+        out_specs=(vmem, hbm),
         scratch_shapes=[
             pltpu.VMEM((3, heads, rows, HD), jnp.bfloat16),
             pltpu.VMEM((n, 2, tiles, 2, TILE, HD), jnp.bfloat16),
@@ -370,17 +381,22 @@
             pltpu.VMEM((3, heads * rows, TILE), jnp.float32),
             pltpu.VMEM((2, rows, q_half), jnp.bfloat16),
             pltpu.VMEM((n, 1, TILE), jnp.int32),
+            pltpu.SMEM(tile_order.shape, jnp.int32),
+            pltpu.SMEM(exit_layer.shape, jnp.int32),
+            pltpu.SMEM((1,), jnp.int32),
             dma((2, 2)),
             dma((2, heads)),
+            dma((3,)),
             dma((n + 1, 2, tiles)),
             dma((n, 2, tiles)),
             dma((tiles + 1,)),
             dma((tiles + 1,)),
             dma((n + 1,)),
             dma((n,)),
+            pltpu.SemaphoreType.REGULAR,
         ],
         compiler_params=pltpu.CompilerParams(
-            collective_id=0, has_side_effects=True, vmem_limit_bytes=64_000_000
+            collective_id=0, has_side_effects=True, vmem_limit_bytes=62_500_000
         ),
         name="attend_line",
     )(

time: 57.2 us -> 53 us (0.927)
  Pallas kernels: 52.7 us -> 49.7 us
  local copies, waits for them, and re-layouts: 2.06 us -> 0.88 us
    pallas_call x1, Pallas kernels: 52.7 us -> 49.7 us  [body(): pl.pallas_call(functools.partial(kernel, n), out_shape=(pltpu.VMEM((rows,...]
    unnamed x1, local copies, waits for them, and re-layouts: 2.06 us -> 0.88 us
where the time goes in v2:
time: 53 us; the launch traced here: 52.9 us
  Pallas kernels  49.7 us (94%)
  between operations  2.33 us (4%)
  local copies, waits for them, and re-layouts  0.88 us (2%)
    pallas_call x1, Pallas kernels, body(): pl.pallas_call(functools.partial(kernel, n), out_shape=(pltpu.VMEM((rows,...  49.7 us

profile of v2, /device:TPU:1, one launch (start us, length us, event | category | flops | bytes accessed | tf_op | source)
XLA Modules:
  0.0 52.9 jit_solution(8916255114459395132)
XLA Ops:
  0.6 49.7 %attend_line.1 = (bf16[384,1024]{1,0:T(8,128)(2,1)S(1)}, s32[1]{0:T(128)}) custom-call(s32[12]{0:T(128)} %order_hbm.1, s32[3]{0:T(128)} %exit_hbm.1, bf16[384,1024]{1,0:T(8,128)(2,1)} %bitcast.5, bf16[3,128,512]{2,1,0:T(8,128)(2,1)} %bitcast.6, bf16[3,128,512]{2,1,0:T(8,128)(2,1)} %bitcast.7), custom_call_target="tpu_custom_call" | custom-call | tf_op jit(solution)/shard_map/attend_line/pallas_call | solution.py:369
  50.3 0.9 %copy.9 = bf16[1,384,1024]{2,1,0:T(8,128)(2,1)} copy(bf16[1,384,1024]{2,1,0:T(8,128)(2,1)S(1)} %bitcast.4) | data formatting | bytes 1572864

commit v3 on v2

--- a/solution.py
+++ b/solution.py
@@ -16,13 +16,13 @@
 OUT_SCALE = SOFTCAP * math.log2(math.e)
 MESH = pl.DeviceIdType.MESH
 SERVED, SPREAD = 0, 1
-GATE_A, GATE_B = 2, 1
+GATE_A, GATE_B, AHEAD = 2, 2, 2
 
 
 def kernel(
     n, order_hbm, exit_hbm, q_hbm, k_hbm, v_hbm, out_ref, live_hbm,
     qb, kv, acc, den, done, exits, order_ref, exit_ref, live_ref, kv_sem, q_sem,
-    small_sem, send_sem, recv_sem, pair_send, pair_recv, exit_send, exit_recv, ready,
+    small_sem, send_sem, recv_sem, pair_send, pair_recv, exit_recv, ready,
 ):
     me = lax.axis_index("seq")
     core = lax.axis_index("head")
@@ -42,18 +42,25 @@
     def peer(step):
         return {"seq": jnp.clip(me + step, 0, far)}
 
-    def own_copy(hh, which):
-        src = (k_hbm, v_hbm)[which]
-        return pltpu.make_async_copy(
-            src.at[:, :, pl.ds(pl.multiple_of(hh * HD, HD), HD)],
-            kv.at[me, hh, :, which],
-            kv_sem.at[hh, which],
-        )
-
-    def own_queries(hh, h):
-        return pltpu.make_async_copy(
-            q_hbm.at[:, pl.ds(hh * q_half + h * HD, HD)], qb.at[hh, h], q_sem.at[hh, h]
-        )
+    def load_own(hh):
+        for which, src in enumerate((k_hbm, v_hbm)):
+            pltpu.make_async_copy(
+                src.at[:, :, pl.ds(pl.multiple_of(hh * HD, HD), HD)],
+                kv.at[me, hh, :, which],
+                kv_sem.at[hh],
+            ).start()
+
+    def wait_own(hh):
+        pltpu.make_async_copy(kv.at[me, hh], kv.at[me, hh], kv_sem.at[hh]).wait()
+
+    def load_queries(hh):
+        for h in range(heads):
+            pltpu.make_async_copy(
+                q_hbm.at[:, pl.ds(hh * q_half + h * HD, HD)], qb.at[hh, h], q_sem.at[hh]
+            ).start()
+
+    def wait_queries(hh):
+        pltpu.make_async_copy(qb.at[hh], qb.at[hh], q_sem.at[hh]).wait()
 
     small = [
         pltpu.make_async_copy(exit_hbm, exit_ref, small_sem.at[0]),
@@ -68,15 +75,12 @@
         pl.semaphore_signal(barrier, inc=1, device_id=peer(1), device_id_type=MESH)
 
     small[0].start()
-    for which in range(2):
-        own_copy(first, which).start()
-    for h in range(heads):
-        own_queries(0, h).start()
-    small[1].start()
-    for which in range(2):
-        own_copy(1 - first, which).start()
-    for h in range(heads):
-        own_queries(1, h).start()
+    load_own(first)
+    asks = at_end & (core == 0)
+
+    @pl.when(asks)
+    def _():
+        load_queries(0)
 
     small[0].wait()
     lane = lax.broadcasted_iota(jnp.int32, (1, TILE), 1)
@@ -90,11 +94,13 @@
         pl.semaphore_wait(barrier, 1)
         pl.semaphore_signal(ready, inc=1, device_id=peer(-1), device_id_type=MESH)
 
+    soon = min(AHEAD, tiles - 1)
+
     def hop(owner, hh, t, step):
         return pltpu.make_async_remote_copy(
             src_ref=kv.at[owner, hh, t],
             dst_ref=kv.at[owner, hh, t],
-            send_sem=send_sem.at[jnp.where((owner == me) & (step < 0), n, owner), hh, t],
+            send_sem=send_sem.at[0, jnp.where(step > 0, 1, 0)],
             recv_sem=recv_sem.at[owner, hh, t],
             device_id=peer(step),
             device_id_type=MESH,
@@ -104,7 +110,7 @@
         return pltpu.make_async_remote_copy(
             src_ref=exits.at[owner],
             dst_ref=exits.at[owner],
-            send_sem=exit_send.at[jnp.where((owner == me) & (step < 0), n, owner)],
+            send_sem=send_sem.at[1, jnp.where(step > 0, 1, 0)],
             recv_sem=exit_recv.at[owner],
             device_id=peer(step),
             device_id_type=MESH,
@@ -119,29 +125,25 @@
         def _():
             hop(owner, hh, t, step).start()
 
-    def send_own(hh, step):
-        @pl.loop(0, tiles)
+    def send_own(hh, step, low=0, high=tiles):
+        @pl.loop(low, high)
         def _(t):
             send(me, hh, t, step)
 
     def query_copy():
         return pltpu.make_async_remote_copy(
             src_ref=qb.at[0], dst_ref=qb.at[2],
-            send_sem=pair_send.at[tiles], recv_sem=pair_recv.at[tiles],
+            send_sem=pair_send.at[0], recv_sem=pair_recv.at[0],
             device_id=peer(inward), device_id_type=MESH,
         )
 
-    def done_copy(t):
-        part = pl.ds(t * TILE, TILE)
+    def done_copy(low, count, last):
+        part = pl.ds(low * TILE, count * TILE)
         return pltpu.make_async_remote_copy(
             src_ref=done.at[0, part], dst_ref=done.at[1, part],
-            send_sem=pair_send.at[t], recv_sem=pair_recv.at[t],
+            send_sem=pair_send.at[1], recv_sem=pair_recv.at[2 if last else 1],
             device_id=peer(-inward), device_id_type=MESH,
         )
-
-    def wait_own(hh):
-        for which in range(2):
-            own_copy(hh, which).wait()
 
     def open_side(step):
         exit_hop(me, step).start()
@@ -155,9 +157,15 @@
             query_copy().start()
             send_own(SERVED, step)
 
+        @pl.when(at_end & (core == 1))
+        def _():
+            send_own(SPREAD, step, 0, soon)
+
+    @pl.when(asks)
+    def _():
+        wait_queries(0)
+
     wait_own(first)
-    for h in range(heads):
-        own_queries(0, h).wait()
 
     @pl.when(inside(me - 1))
     def _():
@@ -168,21 +176,28 @@
         pl.semaphore_wait(ready, 1)
         open_side(1)
 
+    load_own(1 - first)
+    load_queries(1)
+    small[1].start()
+
+    @pl.when(~asks)
+    def _():
+        load_queries(0)
+
     wait_own(1 - first)
 
     @pl.when(~at_end)
     def _():
         send_own(1 - first, -inward)
-
-        @pl.when(core == 1)
-        def _():
-            send_own(SERVED, inward)
 
     acc[...] = jnp.zeros_like(acc)
     den[...] = jnp.zeros_like(den)
 
-    for h in range(heads):
-        own_queries(1, h).wait()
+    @pl.when(~asks)
+    def _():
+        wait_queries(0)
+
+    wait_queries(1)
     small[1].wait()
     ahead = lax.broadcasted_iota(jnp.int32, (TILE, TILE), 1) - lax.broadcasted_iota(
         jnp.int32, (TILE, TILE), 0
@@ -240,68 +255,95 @@
             def _():
                 exit_hop(owner, -side).start()
 
+    def collect(i):
+        here = pl.ds(i * TILE, TILE)
+        out_ref[here, pl.ds(0, q_half)] = live_only(i, done[1, here, :])
+
     early = core == 0
 
-    @pl.loop(0, 2 * far)
+    @pl.loop(0, 3 * far - 1)
     def _(u):
-        hh_in = jnp.where(early, u >= far, (u == 0) | (u > far)).astype(jnp.int32)
-        s_in = jnp.where(
-            u >= far + 1 - early, u - far + 1, jnp.where(early, u + 1, jnp.maximum(u, 1))
-        )
-        hh_out = (u >= far).astype(jnp.int32)
-        s_out = jnp.where(u >= far, u - far + 1, u + early)
+        spread_a = u >= far
+        s_a = jnp.where(spread_a, u - far + 1, u + 1)
+        served_b = (u >= far) & (u < 2 * far)
+        late_b = u >= 2 * far
+        s_b = jnp.where(late_b, u - 2 * far + 2, jnp.where(served_b, u - far + 1, u + 1))
+        hh_in = jnp.where(early, spread_a, ~served_b).astype(jnp.int32)
+        s_in = jnp.where(early, s_a, s_b)
+        extra = serves & (u == far + 1)
+        hh_out = jnp.where(early, spread_a, ~served_b | extra).astype(jnp.int32)
+        s_out = jnp.where(early, s_a, jnp.where(extra, 1, jnp.where(late_b, s_b - 1, s_b)))
+        part_in = ~early & (u > 0) & (hh_in == SPREAD)
+        low_in = jnp.where(part_in & late_b, soon, 0)
+        high_in = jnp.where(part_in & ~late_b, soon, tiles)
+        part_out = ~early & (hh_out == SPREAD)
+        low_out = jnp.where(part_out & (late_b | extra), soon, 0)
+        high_out = jnp.where(part_out & ~(late_b | extra), soon, tiles)
         from_in = me + inward * s_in
         from_out = me - inward * s_out
-        has_in = inside(from_in) & ~(at_end & (hh_in == SERVED))
-        has_out = inside(from_out) & (s_out > 0) & ~at_end
-        serving = serves & (hh_in == SERVED) & inside(from_in)
-
-        @pl.when(has_in | has_out)
+        runs = ~early | (u < 2 * far)
+        any_in = runs & inside(from_in) & ~(at_end & (hh_in == SERVED))
+        any_out = runs & inside(from_out) & ~at_end & ~(late_b & ~early & serves)
+        serving = runs & serves & (hh_in == SERVED) & inside(from_in)
+
+        @pl.when(any_in | any_out)
         def _():
             @pl.loop(0, tiles)
             def _(t):
-                @pl.when((u == 2 * far - 1) & (t == tiles - 1) & at_end)
-                def _():
-                    for i in range(tiles):
-                        here = pl.ds(i * TILE, TILE)
-                        done_copy(i).wait_recv()
-                        out_ref[here, pl.ds(0, q_half)] = live_only(i, done[1, here, :])
+                has_in = any_in & (t >= low_in) & (t < high_in)
+                has_out = any_out & (t >= low_out) & (t < high_out)
+
+                @pl.when((u == jnp.where(early, 2 * far - 1, 3 * far - 2)) & (t == tiles - 1) & at_end)
+                def _():
+                    done_copy(0, tiles - 1, False).wait_recv()
+                    for i in range(tiles - 1):
+                        collect(i)
+
+                @pl.when(has_out)
+                def _():
+                    arrive(from_out, hh_out, t, -inward)
 
                 @pl.when(has_in)
                 def _():
                     arrive(from_in, hh_in, t, inward)
 
-                @pl.when(has_out)
-                def _():
-                    arrive(from_out, hh_out, t, -inward)
+                @pl.when(~early & serves & (u == 2 * far) & (t == tiles - 1))
+                def _():
+                    done_copy(tiles - 1, 1, True).start()
 
                 @pl.when(early & ~at_end & (u == 0) & (t == tiles - 1))
                 def _():
                     send_own(SPREAD, inward)
+
+                @pl.when(~early & ~at_end & (u == 0) & (t == soon - 1))
+                def _():
+                    send_own(SERVED, inward)
 
                 @pl.when(~early & at_end & (u == 0) & (t == GATE_B))
                 def _():
                     query_copy().start()
                     send_own(SERVED, inward)
+                    send_own(SPREAD, inward, soon, tiles)
+
+                @pl.when(early & at_end & (u == far) & (t == GATE_A))
+                def _():
                     send_own(SPREAD, inward)
 
-                @pl.when(early & at_end & (u == far) & (t == GATE_A))
-                def _():
-                    send_own(SPREAD, inward)
-
                 @pl.when(serving & (s_in == 1) & (t == 0))
                 def _():
                     query_copy().wait_recv()
 
-                @pl.loop(jnp.where(has_in, 0, 1), jnp.where(serving, jnp.where(s_in == 1, 5, 3), jnp.where(has_out, 2, 1)))
+                @pl.loop(jnp.where(serving, 0, 3), jnp.where(has_out, 5, 4))
                 def _(k):
-                    owner = jnp.where(k == 4, me, jnp.where((k == 1) | (k == 3), from_out, from_in))
-                    hh = jnp.where(k == 1, hh_out, hh_in)
-
-                    @pl.when(has_out | (k != 1))
+                    owner = jnp.where(
+                        k == 2, me, jnp.where((k == 1) | (k == 4), from_out, from_in)
+                    )
+
+                    @pl.when(jnp.where((k == 1) | (k == 2), s_in == 1, (k != 3) | has_in))
                     def _():
+                        hh = jnp.where(k == 4, hh_out, hh_in)
                         fold_into(
-                            jnp.where(k > 1, 2, hh), jnp.where(k > 1, end, me), owner, hh, t
+                            jnp.where(k < 3, 2, hh), jnp.where(k < 3, end, me), owner, hh, t
                         )
 
         @pl.when(serving & (s_in == far - 1))
@@ -310,10 +352,13 @@
                 for h in range(heads):
                     done[0, pl.ds(t * TILE, TILE), pl.ds(h * HD, HD)] = finish(2, t, h)
                 if t > 0:
-                    done_copy(t - 1).start()
-            for h in range(heads):
-                keep(0, 0, h)
-            done_copy(tiles - 1).start()
+                    done_copy(t - 1, 1, False).start()
+
+            @pl.when(early)
+            def _():
+                for h in range(heads):
+                    keep(0, 0, h)
+                done_copy(tiles - 1, 1, True).start()
 
     live_ref[0] = jnp.sum((exits[...] > 0).astype(jnp.int32))
     result.start()
@@ -330,29 +375,38 @@
 
     @pl.when(at_end)
     def _():
+        done_copy(tiles - 1, 1, True).wait_recv()
+        collect(tiles - 1)
         query_copy().wait_send()
 
     @pl.when(serves)
     def _():
-        for t in range(tiles):
-            done_copy(t).wait_send()
+        done_copy(0, tiles, True).wait_send()
 
     for step in (1, -1):
-        @pl.loop(0, n)
-        def _(s):
-            owner = me - step * s
-
-            @pl.when(inside(owner) & inside(me + step))
+        room = jnp.where(step > 0, far - me, me)
+        count = n - room
+
+        def sent(ref, row):
+            return pltpu.make_async_remote_copy(
+                src_ref=ref, dst_ref=ref,
+                send_sem=send_sem.at[row, (step + 1) // 2], recv_sem=exit_recv.at[0],
+                device_id=peer(step), device_id_type=MESH,
+            )
+
+        @pl.when(room == 1)
+        def _():
+            sent(kv.at[pl.ds(0, far), SPREAD], 0).wait_send()
+
+        for c in range(1, n):
+            @pl.when(count == c)
             def _():
-                exit_hop(owner, step).wait_send()
-
-            @pl.loop(0, 2)
-            def _(hh):
-                @pl.when(inside(owner) & goes(hh, step))
-                def _():
-                    @pl.loop(0, tiles)
-                    def _(t):
-                        hop(owner, hh, t, step).wait_send()
+                sent(exits.at[pl.ds(0, c)], 1).wait_send()
+
+            if c < far:
+                @pl.when(count == c)
+                def _():
+                    sent(kv.at[pl.ds(0, c)], 0).wait_send()
 
     result.wait()
 
@@ -384,14 +438,13 @@
             pltpu.SMEM(tile_order.shape, jnp.int32),
             pltpu.SMEM(exit_layer.shape, jnp.int32),
             pltpu.SMEM((1,), jnp.int32),
+            dma((2,)),
+            dma((2,)),
+            dma((3,)),
             dma((2, 2)),
-            dma((2, heads)),
+            dma((n, 2, tiles)),
+            dma((2,)),
             dma((3,)),
-            dma((n + 1, 2, tiles)),
-            dma((n, 2, tiles)),
-            dma((tiles + 1,)),
-            dma((tiles + 1,)),
-            dma((n + 1,)),
             dma((n,)),
             pltpu.SemaphoreType.REGULAR,
         ],

time: 53 us -> 50.9 us (0.960)
  Pallas kernels: 49.7 us -> 47.5 us
    pallas_call x1, Pallas kernels: 49.7 us -> 47.5 us  [body(): pl.pallas_call(functools.partial(kernel, n), out_shape=(pltpu.VMEM((rows,...]
where the time goes in v3:
time: 50.9 us; the launch traced here: 50.7 us
  Pallas kernels  47.5 us (93%)
  between operations  2.33 us (5%)
  local copies, waits for them, and re-layouts  0.88 us (2%)
    pallas_call x1, Pallas kernels, body(): pl.pallas_call(functools.partial(kernel, n), out_shape=(pltpu.VMEM((rows,...  47.5 us

profile of v3, /device:TPU:1, one launch (start us, length us, event | category | flops | bytes accessed | tf_op | source)
XLA Modules:
  0.0 50.7 jit_solution(11275640026825849041)
XLA Ops:
  0.6 47.5 %attend_line.1 = (bf16[384,1024]{1,0:T(8,128)(2,1)S(1)}, s32[1]{0:T(128)}) custom-call(s32[12]{0:T(128)} %order_hbm.1, s32[3]{0:T(128)} %exit_hbm.1, bf16[384,1024]{1,0:T(8,128)(2,1)} %bitcast.5, bf16[3,128,512]{2,1,0:T(8,128)(2,1)} %bitcast.6, bf16[3,128,512]{2,1,0:T(8,128)(2,1)} %bitcast.7), custom_call_target="tpu_custom_call" | custom-call | tf_op jit(solution)/shard_map/attend_line/pallas_call | solution.py:423
  48.2 0.9 %copy.9 = bf16[1,384,1024]{2,1,0:T(8,128)(2,1)} copy(bf16[1,384,1024]{2,1,0:T(8,128)(2,1)S(1)} %bitcast.4) | data formatting | bytes 1572864

commit v4 on v3

--- a/solution.py
+++ b/solution.py
@@ -16,7 +16,7 @@
 OUT_SCALE = SOFTCAP * math.log2(math.e)
 MESH = pl.DeviceIdType.MESH
 SERVED, SPREAD = 0, 1
-GATE_A, GATE_B, AHEAD = 2, 2, 2
+GATE_A, GATE_B, AHEAD = 2, 2, 1
 
 
 def kernel(
@@ -258,6 +258,19 @@
     def collect(i):
         here = pl.ds(i * TILE, TILE)
         out_ref[here, pl.ds(0, q_half)] = live_only(i, done[1, here, :])
+
+    def finish_served():
+        for t in range(tiles):
+            for h in range(heads):
+                done[0, pl.ds(t * TILE, TILE), pl.ds(h * HD, HD)] = finish(2, t, h)
+            if t > 0:
+                done_copy(t - 1, 1, False).start()
+
+        @pl.when(core == 0)
+        def _():
+            for h in range(heads):
+                keep(0, 0, h)
+            done_copy(tiles - 1, 1, True).start()
 
     early = core == 0
 
@@ -284,6 +297,8 @@
         runs = ~early | (u < 2 * far)
         any_in = runs & inside(from_in) & ~(at_end & (hh_in == SERVED))
         any_out = runs & inside(from_out) & ~at_end & ~(late_b & ~early & serves)
+        later = early & ~at_end & (hh_in == SERVED)
+        both = early & ~at_end & (hh_in == SPREAD)
         serving = runs & serves & (hh_in == SERVED) & inside(from_in)
 
         @pl.when(any_in | any_out)
@@ -333,32 +348,23 @@
                 def _():
                     query_copy().wait_recv()
 
-                @pl.loop(jnp.where(serving, 0, 3), jnp.where(has_out, 5, 4))
+                @pl.loop(0, jnp.where(serving, jnp.where(s_in == 1, 3, 1), 0))
                 def _(k):
-                    owner = jnp.where(
-                        k == 2, me, jnp.where((k == 1) | (k == 4), from_out, from_in)
-                    )
-
-                    @pl.when(jnp.where((k == 1) | (k == 2), s_in == 1, (k != 3) | has_in))
+                    owner = jnp.where(k == 2, me, jnp.where(k == 1, from_out, from_in))
+                    fold_into(2, end, owner, SERVED, t)
+
+                @pl.when(serving & (s_in == far - 1) & (t == tiles - 1))
+                def _():
+                    finish_served()
+
+                @pl.loop(jnp.where(has_in, 0, 1), jnp.where(both, 4, 2))
+                def _(k):
+                    outer = (k % 2) == 1
+
+                    @pl.when(jnp.where(outer, has_out, has_in) & ~later)
                     def _():
-                        hh = jnp.where(k == 4, hh_out, hh_in)
-                        fold_into(
-                            jnp.where(k < 3, 2, hh), jnp.where(k < 3, end, me), owner, hh, t
-                        )
-
-        @pl.when(serving & (s_in == far - 1))
-        def _():
-            for t in range(tiles):
-                for h in range(heads):
-                    done[0, pl.ds(t * TILE, TILE), pl.ds(h * HD, HD)] = finish(2, t, h)
-                if t > 0:
-                    done_copy(t - 1, 1, False).start()
-
-            @pl.when(early)
-            def _():
-                for h in range(heads):
-                    keep(0, 0, h)
-                done_copy(tiles - 1, 1, True).start()
+                        hh = jnp.where(k > 1, SERVED, jnp.where(outer, hh_out, hh_in))
+                        fold_into(hh, me, jnp.where(outer, from_out, from_in), hh, t)
 
     live_ref[0] = jnp.sum((exits[...] > 0).astype(jnp.int32))
     result.start()

time: 50.9 us -> 50.2 us (0.986)
  Pallas kernels: 47.5 us -> 46.8 us
    pallas_call x1, Pallas kernels: 47.5 us -> 46.8 us  [body(): pl.pallas_call(functools.partial(kernel, n), out_shape=(pltpu.VMEM((rows,...]
where the time goes in v4:
time: 50.2 us; the launch traced here: 50 us
  Pallas kernels  46.8 us (93%)
  between operations  2.33 us (5%)
  local copies, waits for them, and re-layouts  0.88 us (2%)
    pallas_call x1, Pallas kernels, body(): pl.pallas_call(functools.partial(kernel, n), out_shape=(pltpu.VMEM((rows,...  46.8 us

profile of v4, /device:TPU:1, one launch (start us, length us, event | category | flops | bytes accessed | tf_op | source)
XLA Modules:
  0.0 50.0 jit_solution(14622505459328048362)
XLA Ops:
  0.6 46.8 %attend_line.1 = (bf16[384,1024]{1,0:T(8,128)(2,1)S(1)}, s32[1]{0:T(128)}) custom-call(s32[12]{0:T(128)} %order_hbm.1, s32[3]{0:T(128)} %exit_hbm.1, bf16[384,1024]{1,0:T(8,128)(2,1)} %bitcast.5, bf16[3,128,512]{2,1,0:T(8,128)(2,1)} %bitcast.6, bf16[3,128,512]{2,1,0:T(8,128)(2,1)} %bitcast.7), custom_call_target="tpu_custom_call" | custom-call | tf_op jit(solution)/shard_map/attend_line/pallas_call | solution.py:429
  47.4 0.9 %copy.9 = bf16[1,384,1024]{2,1,0:T(8,128)(2,1)} copy(bf16[1,384,1024]{2,1,0:T(8,128)(2,1)S(1)} %bitcast.4) | data formatting | bytes 1572864

commit v5 on v4

--- a/solution.py
+++ b/solution.py
@@ -20,8 +20,8 @@
 
 
 def kernel(
-    n, order_hbm, exit_hbm, q_hbm, k_hbm, v_hbm, out_ref, live_hbm,
-    qb, kv, acc, den, done, exits, order_ref, exit_ref, live_ref, kv_sem, q_sem,
+    n, order_hbm, exit_hbm, q_hbm, k_hbm, v_hbm, out_ref, exits,
+    qb, kv, acc, den, done, order_ref, exit_ref, kv_sem, q_sem,
     small_sem, send_sem, recv_sem, pair_send, pair_recv, exit_recv, ready,
 ):
     me = lax.axis_index("seq")
@@ -66,7 +66,6 @@
         pltpu.make_async_copy(exit_hbm, exit_ref, small_sem.at[0]),
         pltpu.make_async_copy(order_hbm, order_ref, small_sem.at[1]),
     ]
-    result = pltpu.make_async_copy(live_ref, live_hbm, small_sem.at[2])
 
     barrier = pltpu.get_barrier_semaphore()
 
@@ -366,9 +365,6 @@
                         hh = jnp.where(k > 1, SERVED, jnp.where(outer, hh_out, hh_in))
                         fold_into(hh, me, jnp.where(outer, from_out, from_in), hh, t)
 
-    live_ref[0] = jnp.sum((exits[...] > 0).astype(jnp.int32))
-    result.start()
-
     for i in range(tiles):
         for h in range(heads):
             keep(1, i, h)
@@ -414,7 +410,15 @@
                 def _():
                     sent(kv.at[pl.ds(0, c)], 0).wait_send()
 
-    result.wait()
+
+def write_out(attended, exits, out_hbm, live_hbm, live, sems):
+    whole = pltpu.make_async_copy(attended, out_hbm.at[0], sems.at[0])
+    whole.start()
+    live[0] = jnp.sum((exits[...] > 0).astype(jnp.int32))
+    count = pltpu.make_async_copy(live, live_hbm, sems.at[1])
+    count.start()
+    count.wait()
+    whole.wait()
 
 
 def body(n, queries, keys, values, exit_layer, tile_order):
@@ -426,27 +430,25 @@
     hbm = pl.BlockSpec(memory_space=pltpu.HBM)
     vmem = pl.BlockSpec(memory_space=pltpu.VMEM)
     dma = pltpu.SemaphoreType.DMA
-    attended, live = pl.pallas_call(
+    attended, exits = pl.pallas_call(
         functools.partial(kernel, n),
         out_shape=(
             pltpu.VMEM((rows, q_width), jnp.bfloat16),
-            jax.ShapeDtypeStruct((1,), jnp.int32),
+            pltpu.VMEM((n, 1, TILE), jnp.int32),
         ),
         in_specs=[hbm] * 5,
-        out_specs=(vmem, hbm),
+        out_specs=(vmem, vmem),
         scratch_shapes=[
             pltpu.VMEM((3, heads, rows, HD), jnp.bfloat16),
             pltpu.VMEM((n, 2, tiles, 2, TILE, HD), jnp.bfloat16),
             pltpu.VMEM((3, heads * rows, HD), jnp.float32),
             pltpu.VMEM((3, heads * rows, TILE), jnp.float32),
             pltpu.VMEM((2, rows, q_half), jnp.bfloat16),
-            pltpu.VMEM((n, 1, TILE), jnp.int32),
             pltpu.SMEM(tile_order.shape, jnp.int32),
             pltpu.SMEM(exit_layer.shape, jnp.int32),
-            pltpu.SMEM((1,), jnp.int32),
             dma((2,)),
             dma((2,)),
-            dma((3,)),
+            dma((2,)),
             dma((2, 2)),
             dma((n, 2, tiles)),
             dma((2,)),
@@ -455,14 +457,25 @@
             pltpu.SemaphoreType.REGULAR,
         ],
         compiler_params=pltpu.CompilerParams(
-            collective_id=0, has_side_effects=True, vmem_limit_bytes=62_500_000
+            collective_id=0, has_side_effects=True, vmem_limit_bytes=62_000_000
         ),
         name="attend_line",
     )(
         tile_order, exit_layer, queries[0],
         keys.reshape(tiles, TILE, kv_width), values.reshape(tiles, TILE, kv_width),
     )
-    return attended[None], live
+    return pl.pallas_call(
+        write_out,
+        out_shape=(
+            jax.ShapeDtypeStruct((1, rows, q_width), jnp.bfloat16),
+            jax.ShapeDtypeStruct((1,), jnp.int32),
+        ),
+        in_specs=[vmem, vmem],
+        out_specs=(hbm, hbm),
+        scratch_shapes=[pltpu.SMEM((1,), jnp.int32), dma((2,))],
+        compiler_params=pltpu.CompilerParams(vmem_limit_bytes=1_000_000),
+        name="write_out",
+    )(attended, exits)
 
 
 def solution(mesh):

time: 50.2 us -> 48.5 us (0.966)
  between operations: 2.33 us -> 0.64 us
  Pallas kernels: 46.8 us -> 47.7 us
  local copies, waits for them, and re-layouts: 0.88 us -> 0 us
    pallas_call x0 -> x1, Pallas kernels: none -> 0.9 us  [body(): pl.pallas_call(write_out, out_shape=(jax.ShapeDtypeStruct((1, rows, q_wid...]
    unnamed x1 -> x0, local copies, waits for them, and re-layouts: 0.88 us -> none
where the time goes in v5:
time: 48.5 us; the launch traced here: 48.3 us
  Pallas kernels  47.7 us (98%)
  between operations  0.64 us (1%)
    pallas_call x1, Pallas kernels, body(): pl.pallas_call(functools.partial(kernel, n), out_shape=(pltpu.VMEM((rows,...  46.8 us

profile of v5, /device:TPU:1, one launch (start us, length us, event | category | flops | bytes accessed | tf_op | source)
XLA Modules:
  0.0 48.3 jit_solution(2564001416456579555)
XLA Ops:
  0.6 46.8 %attend_line.1 = (bf16[384,1024]{1,0:T(8,128)(2,1)S(1)}, s32[4,1,128]{2,1,0:T(1,128)S(1)}) custom-call(s32[12]{0:T(128)} %order_hbm.1, s32[3]{0:T(128)} %exit_hbm.1, bf16[384,1024]{1,0:T(8,128)(2,1)} %bitcast.3, bf16[3,128,512]{2,1,0:T(8,128)(2,1)} %bitcast.4, bf16[3,128,512]{2,1,0:T(8,128)(2,1)} %bitcast.5), custom_call_target="tpu_custom_call" | custom-call | tf_op jit(solution)/shard_map/attend_line/pallas_call | solution.py:433
  47.4 0.9 %write_out.1 = (bf16[1,384,1024]{2,1,0:T(8,128)(2,1)}, s32[1]{0:T(128)}) custom-call(bf16[384,1024]{1,0:T(8,128)(2,1)S(1)} %get-tuple-element.4.attended, s32[4,1,128]{2,1,0:T(1,128)S(1)} %get-tuple-element.5.exits), custom_call_target="tpu_custom_call" | custom-call | tf_op jit(solution)/shard_map/write_out/pallas_call | solution.py:467

commit v6 on v5

--- a/solution.py
+++ b/solution.py
@@ -42,16 +42,18 @@
     def peer(step):
         return {"seq": jnp.clip(me + step, 0, far)}
 
-    def load_own(hh):
+    def load_own(hh, low, high, sem):
+        here = pl.ds(low, high - low)
         for which, src in enumerate((k_hbm, v_hbm)):
             pltpu.make_async_copy(
-                src.at[:, :, pl.ds(pl.multiple_of(hh * HD, HD), HD)],
-                kv.at[me, hh, :, which],
-                kv_sem.at[hh],
+                src.at[here, :, pl.ds(pl.multiple_of(hh * HD, HD), HD)],
+                kv.at[me, hh, here, which],
+                kv_sem.at[sem],
             ).start()
 
-    def wait_own(hh):
-        pltpu.make_async_copy(kv.at[me, hh], kv.at[me, hh], kv_sem.at[hh]).wait()
+    def wait_own(hh, low, high, sem):
+        part = kv.at[me, hh, pl.ds(low, high - low)]
+        pltpu.make_async_copy(part, part, kv_sem.at[sem]).wait()
 
     def load_queries(hh):
         for h in range(heads):
@@ -73,21 +75,15 @@
     def _():
         pl.semaphore_signal(barrier, inc=1, device_id=peer(1), device_id_type=MESH)
 
+    load_own(first, 0, 1, 2)
     small[0].start()
-    load_own(first)
     asks = at_end & (core == 0)
 
     @pl.when(asks)
     def _():
         load_queries(0)
 
-    small[0].wait()
-    lane = lax.broadcasted_iota(jnp.int32, (1, TILE), 1)
-    mine = jnp.zeros((1, TILE), jnp.int32)
-    for i in range(tiles):
-        mine = jnp.where(lane == i, exit_ref[i], mine)
-    exits[me] = mine
-
+    load_own(first, 1, tiles, first)
     @pl.when(inside(me - 1))
     def _():
         pl.semaphore_wait(barrier, 1)
@@ -144,38 +140,55 @@
             device_id=peer(-inward), device_id_type=MESH,
         )
 
-    def open_side(step):
-        exit_hop(me, step).start()
-
+    def push(step, low, high):
         @pl.when(~at_end)
         def _():
-            send_own(first, step)
-
-        @pl.when(at_end & (core == 0))
-        def _():
-            query_copy().start()
-            send_own(SERVED, step)
-
-        @pl.when(at_end & (core == 1))
-        def _():
-            send_own(SPREAD, step, 0, soon)
+            send_own(first, step, low, high)
+
+        @pl.when(asks)
+        def _():
+            if low == 0:
+                query_copy().start()
+            send_own(SERVED, step, low, high)
 
     @pl.when(asks)
     def _():
         wait_queries(0)
 
-    wait_own(first)
+    wait_own(first, 0, 1, 2)
 
     @pl.when(inside(me - 1))
     def _():
-        open_side(-1)
+        push(-1, 0, 1)
+
+    small[0].wait()
+    lane = lax.broadcasted_iota(jnp.int32, (1, TILE), 1)
+    mine = jnp.zeros((1, TILE), jnp.int32)
+    for i in range(tiles):
+        mine = jnp.where(lane == i, exit_ref[i], mine)
+    exits[me] = mine
+
+    @pl.when(inside(me - 1))
+    def _():
+        exit_hop(me, -1).start()
+
+    wait_own(first, 1, tiles, first)
+
+    @pl.when(inside(me - 1))
+    def _():
+        push(-1, 1, tiles)
 
     @pl.when(inside(me + 1))
     def _():
         pl.semaphore_wait(ready, 1)
-        open_side(1)
-
-    load_own(1 - first)
+        exit_hop(me, 1).start()
+        push(1, 0, tiles)
+
+    @pl.when(at_end & (core == 1))
+    def _():
+        send_own(SPREAD, inward, 0, soon)
+
+    load_own(1 - first, 0, tiles, 1 - first)
     load_queries(1)
     small[1].start()
 
@@ -183,7 +196,7 @@
     def _():
         load_queries(0)
 
-    wait_own(1 - first)
+    wait_own(1 - first, 0, tiles, 1 - first)
 
     @pl.when(~at_end)
     def _():
@@ -446,7 +459,7 @@
             pltpu.VMEM((2, rows, q_half), jnp.bfloat16),
             pltpu.SMEM(tile_order.shape, jnp.int32),
             pltpu.SMEM(exit_layer.shape, jnp.int32),
-            dma((2,)),
+            dma((3,)),
             dma((2,)),
             dma((2,)),
             dma((2, 2)),

time: 48.5 us -> 47.9 us (0.988)
  Pallas kernels: 47.7 us -> 47.1 us
    pallas_call x1, Pallas kernels: 46.8 us -> 46.2 us  [body(): pl.pallas_call(functools.partial(kernel, n), out_shape=(pltpu.VMEM((rows,...]
where the time goes in v6:
time: 47.9 us; the launch traced here: 47.8 us
  Pallas kernels  47.1 us (98%)
  between operations  0.64 us (1%)
    pallas_call x1, Pallas kernels, body(): pl.pallas_call(functools.partial(kernel, n), out_shape=(pltpu.VMEM((rows,...  46.2 us

profile of v6, /device:TPU:1, one launch (start us, length us, event | category | flops | bytes accessed | tf_op | source)
XLA Modules:
  0.0 47.8 jit_solution(16488302793025783241)
XLA Ops:
  0.6 46.2 %attend_line.1 = (bf16[384,1024]{1,0:T(8,128)(2,1)S(1)}, s32[4,1,128]{2,1,0:T(1,128)S(1)}) custom-call(s32[12]{0:T(128)} %order_hbm.1, s32[3]{0:T(128)} %exit_hbm.1, bf16[384,1024]{1,0:T(8,128)(2,1)} %bitcast.3, bf16[3,128,512]{2,1,0:T(8,128)(2,1)} %bitcast.4, bf16[3,128,512]{2,1,0:T(8,128)(2,1)} %bitcast.5), custom_call_target="tpu_custom_call" | custom-call | tf_op jit(solution)/shard_map/attend_line/pallas_call | solution.py:446
  46.9 0.9 %write_out.1 = (bf16[1,384,1024]{2,1,0:T(8,128)(2,1)}, s32[1]{0:T(128)}) custom-call(bf16[384,1024]{1,0:T(8,128)(2,1)S(1)} %get-tuple-element.4.attended, s32[4,1,128]{2,1,0:T(1,128)S(1)} %get-tuple-element.5.exits), custom_call_target="tpu_custom_call" | custom-call | tf_op jit(solution)/shard_map/write_out/pallas_call | solution.py:480

commit v7 on v6

--- a/solution.py
+++ b/solution.py
@@ -16,7 +16,7 @@
 OUT_SCALE = SOFTCAP * math.log2(math.e)
 MESH = pl.DeviceIdType.MESH
 SERVED, SPREAD = 0, 1
-GATE_A, GATE_B, AHEAD = 2, 2, 1
+AHEAD = 1
 
 
 def kernel(
@@ -271,12 +271,31 @@
         here = pl.ds(i * TILE, TILE)
         out_ref[here, pl.ds(0, q_half)] = live_only(i, done[1, here, :])
 
-    def finish_served():
-        for t in range(tiles):
+    def finish_served(owner, t):
+        key_place = order_ref[owner * tiles + t]
+        for i in range(tiles):
+            place = order_ref[end * tiles + i]
+            part = pl.ds(i * TILE, TILE)
+            scores = lax.dot_general(
+                qb[2, :, part, :].reshape(heads * TILE, HD), kv[owner, SERVED, t, 0],
+                (((1,), (1,)), ((), ())), preferred_element_type=jnp.float32,
+            ).reshape(heads, TILE, TILE)
+            weights = jnp.where(
+                (ahead - (place - key_place) * TILE)[None] <= 0,
+                jnp.exp2(OUT_SCALE * jnp.tanh(scores * IN_SCALE)), 0.0,
+            )
+            added = jnp.dot(
+                weights.astype(jnp.bfloat16).reshape(heads * TILE, TILE),
+                kv[owner, SERVED, t, 1], preferred_element_type=jnp.float32,
+            ).reshape(heads, TILE, HD)
             for h in range(heads):
-                done[0, pl.ds(t * TILE, TILE), pl.ds(h * HD, HD)] = finish(2, t, h)
-            if t > 0:
-                done_copy(t - 1, 1, False).start()
+                here = pl.ds(h * rows + i * TILE, TILE)
+                total = jnp.sum(den[2, here, :] + weights[h], axis=1, keepdims=True)
+                done[0, part, pl.ds(h * HD, HD)] = (
+                    (acc[2, here, :] + added[h]) / total
+                ).astype(jnp.bfloat16)
+            if i > 0:
+                done_copy(i - 1, 1, False).start()
 
         @pl.when(core == 0)
         def _():
@@ -346,13 +365,13 @@
                 def _():
                     send_own(SERVED, inward)
 
-                @pl.when(~early & at_end & (u == 0) & (t == GATE_B))
+                @pl.when(~early & at_end & (u == 0) & (t == tiles - 1))
                 def _():
                     query_copy().start()
                     send_own(SERVED, inward)
                     send_own(SPREAD, inward, soon, tiles)
 
-                @pl.when(early & at_end & (u == far) & (t == GATE_A))
+                @pl.when(early & at_end & (u == far) & (t == tiles - 1))
                 def _():
                     send_own(SPREAD, inward)
 
@@ -360,14 +379,16 @@
                 def _():
                     query_copy().wait_recv()
 
-                @pl.loop(0, jnp.where(serving, jnp.where(s_in == 1, 3, 1), 0))
+                final = serving & (s_in == far - 1) & (t == tiles - 1)
+
+                @pl.loop(0, jnp.where(serving & ~final, jnp.where(s_in == 1, 3, 1), 0))
                 def _(k):
                     owner = jnp.where(k == 2, me, jnp.where(k == 1, from_out, from_in))
                     fold_into(2, end, owner, SERVED, t)
 
-                @pl.when(serving & (s_in == far - 1) & (t == tiles - 1))
-                def _():
-                    finish_served()
+                @pl.when(final)
+                def _():
+                    finish_served(from_in, t)
 
                 @pl.loop(jnp.where(has_in, 0, 1), jnp.where(both, 4, 2))
                 def _(k):

time: 47.9 us -> 47.9 us (level)
  no operation moved by 1% of the time
where the time goes in v7:
time: 47.9 us; the launch traced here: 47.8 us
  Pallas kernels  47.1 us (98%)
  between operations  0.64 us (1%)
    pallas_call x1, Pallas kernels, body(): pl.pallas_call(functools.partial(kernel, n), out_shape=(pltpu.VMEM((rows,...  46.2 us

profile of v7, /device:TPU:1, one launch (start us, length us, event | category | flops | bytes accessed | tf_op | source)
XLA Modules:
  0.0 47.8 jit_solution(6992327384873205638)
XLA Ops:
  0.6 46.2 %attend_line.1 = (bf16[384,1024]{1,0:T(8,128)(2,1)S(1)}, s32[4,1,128]{2,1,0:T(1,128)S(1)}) custom-call(s32[12]{0:T(128)} %order_hbm.1, s32[3]{0:T(128)} %exit_hbm.1, bf16[384,1024]{1,0:T(8,128)(2,1)} %bitcast.3, bf16[3,128,512]{2,1,0:T(8,128)(2,1)} %bitcast.4, bf16[3,128,512]{2,1,0:T(8,128)(2,1)} %bitcast.5), custom_call_target="tpu_custom_call" | custom-call | tf_op jit(solution)/shard_map/attend_line/pallas_call | solution.py:467
  46.9 0.9 %write_out.1 = (bf16[1,384,1024]{2,1,0:T(8,128)(2,1)}, s32[1]{0:T(128)}) custom-call(bf16[384,1024]{1,0:T(8,128)(2,1)S(1)} %get-tuple-element.4.attended, s32[4,1,128]{2,1,0:T(1,128)S(1)} %get-tuple-element.5.exits), custom_call_target="tpu_custom_call" | custom-call | tf_op jit(solution)/shard_map/write_out/pallas_call | solution.py:501

commit v8 on v7

--- a/solution.py
+++ b/solution.py
@@ -217,23 +217,22 @@
 
     def fold_into(slot, row_owner, owner, hh, t):
         key_place = order_ref[owner * tiles + t]
-        over = jnp.stack(
-            [
-                ahead - (order_ref[row_owner * tiles + i] - key_place) * TILE
-                for i in range(tiles)
-            ]
-        )
-        stacked = (heads * rows, HD)
-        scores = lax.dot_general(
-            qb[slot].reshape(stacked), kv[owner, hh, t, 0],
-            (((1,), (1,)), ((), ())), preferred_element_type=jnp.float32,
-        ).reshape(heads, tiles, TILE, TILE)
-        weights = jnp.where(
-            over[None] <= 0, jnp.exp2(OUT_SCALE * jnp.tanh(scores * IN_SCALE)), 0.0
-        ).reshape(heads * rows, TILE)
-        den[slot] += weights
+        parts = []
+        for h in range(heads):
+            for i in range(tiles):
+                here = pl.ds(h * rows + i * TILE, TILE)
+                gap = (order_ref[row_owner * tiles + i] - key_place) * TILE
+                scores = lax.dot_general(
+                    qb[slot, h, pl.ds(i * TILE, TILE), :], kv[owner, hh, t, 0],
+                    (((1,), (1,)), ((), ())), preferred_element_type=jnp.float32,
+                )
+                weights = jnp.where(
+                    ahead <= gap, jnp.exp2(OUT_SCALE * jnp.tanh(scores * IN_SCALE)), 0.0
+                )
+                den[slot, here, :] += weights
+                parts.append(weights.astype(jnp.bfloat16))
         acc[slot] += jnp.dot(
-            weights.astype(jnp.bfloat16), kv[owner, hh, t, 1],
+            jnp.concatenate(parts, axis=0), kv[owner, hh, t, 1],
             preferred_element_type=jnp.float32,
         )
 

time: 47.9 us -> 47.9 us (level)
  no operation moved by 1% of the time
where the time goes in v8:
time: 47.9 us; the launch traced here: 47.8 us
  Pallas kernels  47.1 us (98%)
  between operations  0.64 us (1%)
    pallas_call x1, Pallas kernels, body(): pl.pallas_call(functools.partial(kernel, n), out_shape=(pltpu.VMEM((rows,...  46.2 us

profile of v8, /device:TPU:1, one launch (start us, length us, event | category | flops | bytes accessed | tf_op | source)
XLA Modules:
  0.0 47.8 jit_solution(2482162389499476064)
XLA Ops:
  0.6 46.2 %attend_line.1 = (bf16[384,1024]{1,0:T(8,128)(2,1)S(1)}, s32[4,1,128]{2,1,0:T(1,128)S(1)}) custom-call(s32[12]{0:T(128)} %order_hbm.1, s32[3]{0:T(128)} %exit_hbm.1, bf16[384,1024]{1,0:T(8,128)(2,1)} %bitcast.3, bf16[3,128,512]{2,1,0:T(8,128)(2,1)} %bitcast.4, bf16[3,128,512]{2,1,0:T(8,128)(2,1)} %bitcast.5), custom_call_target="tpu_custom_call" | custom-call | tf_op jit(solution)/shard_map/attend_line/pallas_call | solution.py:466
  46.9 0.9 %write_out.1 = (bf16[1,384,1024]{2,1,0:T(8,128)(2,1)}, s32[1]{0:T(128)}) custom-call(bf16[384,1024]{1,0:T(8,128)(2,1)S(1)} %get-tuple-element.4.attended, s32[4,1,128]{2,1,0:T(1,128)S(1)} %get-tuple-element.5.exits), custom_call_target="tpu_custom_call" | custom-call | tf_op jit(solution)/shard_map/write_out/pallas_call | solution.py:500
